TPU v7x, 8 devices: a whole 2x2x1 slice. The times are simulated.
8 devices in a mesh: dp: 2 (over y, z), tp: 4 (over x, core).
Axes of the slice: x: 2, y: 2, z: 1, core: 2. Of those that a mesh axis runs over, the one named last changes fastest.
Arguments:
- x: bfloat16 [4096, 4096], P('dp'), parts along dimension 0
- w_gate: bfloat16 [4096, 14336], P(None, 'tp')
- w_up: bfloat16 [4096, 14336], P(None, 'tp')
- w_down: bfloat16 [14336, 4096], P('tp')
Outputs:
- output: bfloat16 [4096, 4096], P('dp'), parts along dimension 0
There are 2 independent parts. A program takes and returns all parts, laid end to end along the dimension named above; an argument that names none is the same for every part.
All inputs are finite; a program needn't handle non-finite values.
Results may differ from a plain program's by a relative error of at most 0.016.
Values are sent between devices in bfloat16 or wider.
A program may use at most 2 GiB of HBM per device.

v0:
```python
import jax
import jax.numpy as jnp
from jax import lax
from jax.sharding import PartitionSpec as P


def solution(mesh):
    def step(x, w_gate, w_up, w_down):
        gate = jnp.dot(x, w_gate, preferred_element_type=jnp.float32)
        up = jnp.dot(x, w_up, preferred_element_type=jnp.float32)
        hidden = (jax.nn.silu(gate) * up).astype(jnp.bfloat16)
        term = jnp.dot(hidden, w_down, preferred_element_type=jnp.float32).astype(jnp.bfloat16)
        return lax.psum(term, "tp")

    return jax.shard_map(
        step,
        mesh=mesh,
        in_specs=(P("dp", None), P(None, "tp"), P(None, "tp"), P("tp", None)),
        out_specs=P("dp", None),
        check_vma=False,
    )
```

profile of v0, /device:TPU:0, one launch (start us, length us, event | category | flops | bytes accessed | tf_op | source)
XLA Modules:
  0.0 531.2 jit_solution(7498807341972379187)
XLA Ops:
  6.5 0.0 all-reduce.2.cloned.1.call-start
  6.5 71.3 %fusion = f32[2048,3584]{1,0:T(8,128)} fusion(bf16[2048,4096]{1,0:T(8,128)(2,1)} %param.4, bf16[4096,3584]{1,0:T(8,128)(2,1)} %param.5), kind=kOutput, calls=%fused_computation.2 | convolution fusion | flops 60129542144 | bytes 75497472 | tf_op jit(solution)/shard_map/dot_general | solution.py:9
  77.8 76.9 %multiply_convert_fusion = bf16[2048,3584]{1,0:T(8,128)(2,1)} fusion(f32[2048,3584]{1,0:T(8,128)} %fusion, bf16[2048,4096]{1,0:T(8,128)(2,1)} %param.4, bf16[4096,3584]{1,0:T(8,128)(2,1)} %param.6), kind=kOutput, calls=%fused_computation | convolution fusion | flops 60173582336 | bytes 90177536 | tf_op jit(solution)/shard_map/dot_general | solution.py:10
  154.7 70.1 %convolution_convert_fusion = bf16[2048,4096]{1,0:T(8,128)(2,1)} fusion(bf16[2048,3584]{1,0:T(8,128)(2,1)} %multiply_convert_fusion, bf16[3584,4096]{1,0:T(8,128)(2,1)} %param.7), kind=kOutput, calls=%fused_computation.1 | convolution fusion | flops 60137930752 | bytes 60817408 | tf_op jit(solution)/shard_map/dot_general | solution.py:12
  224.8 0.0 all-reduce.2.cloned.1.call-update
  224.8 285.5 %all-reduce.2.cloned.1.call-done = bf16[2048,4096]{1,0:T(8,128)(2,1)} async-done(((bf16[2048,4096]{1,0:T(8,128)(2,1)}), bf16[2048,4096]{1,0:T(8,128)(2,1)}) %all-reduce.2.cloned.1.call-update) | async-done | bytes 16777232 | tf_op jit(solution)/shard_map/psum | solution.py:13
  510.3 14.1 %copy.6 = bf16[2048,4096]{1,0:T(8,128)(2,1)} copy(bf16[2048,4096]{1,0:T(8,128)(2,1)} %all-reduce.2.cloned.1.call-done) | data formatting | bytes 33554432
Async XLA Ops:
  6.5 503.8 %all-reduce.2.cloned.1.call-start = ((), (), s32[]{:S(2)}) async-start(), calls=%async_computation | async-start | bytes 33554432 | tf_op jit(solution)/shard_map/psum | solution.py:13
Sparse Core Ops, SparseCore 0:
  224.9 285.3 all-reduce.1
where the time goes:
time: 531 us
  waiting for transfers between devices  286 us (54%)
  matrix products  218 us (41%)
  local copies, waits for them, and re-layouts  14.1 us (3%)
  between operations  13.4 us (3%)
    psum x1, waiting for transfers between devices, step(): return lax.psum(term, 'tp')  286 us
    dot_general x1, matrix products, step(): up = jnp.dot(x, w_up, preferred_element_type=jnp.float32)  76.9 us
    dot_general x1, matrix products, step(): gate = jnp.dot(x, w_gate, preferred_element_type=jnp.float32)  71.3 us
    dot_general x1, matrix products, step(): jnp.dot(hidden, w_down, preferred_element_type=jnp.float32)  70.1 us
    unnamed x1, local copies, waits for them, and re-layouts  14.1 us
  transfers between devices with their start and end apart: 1, of which 1 were waited for; matrix products, arithmetic and copies ran while one was open for 0% of the time, Pallas kernels for 0%

commit v1 on v0

v1 whole, which is shorter than its diff:
```python
import functools

import jax
import jax.numpy as jnp
from jax import lax
from jax.experimental import pallas as pl
from jax.experimental.pallas import tpu as pltpu
from jax.sharding import PartitionSpec as P

MESH = pl.DeviceIdType.MESH
BF16, F32 = jnp.bfloat16, jnp.float32
CHUNKS = (512, 640, 640, 256)
COLS = 512
TILES = 8


def kernel(
    x_hbm, wg_hbm, wu_hbm, wd_hbm, y_hbm,
    xb, wb, hid, own, out_a, in_a, out_b, in_b, yb,
    xsem, wsem, sa, ra, sb, rb, sy, ry, ly,
):
    depth, ff = wg_hbm.shape
    ups = ff // COLS
    dp, tp = lax.axis_index("dp"), lax.axis_index("tp")
    chip, core = tp // 2, tp % 2
    sibling = (dp, 2 * chip + 1 - core)
    partner = (dp, 2 * (1 - chip) + core)
    starts = [sum(CHUNKS[:i]) for i in range(len(CHUNKS))]
    last = len(CHUNKS) - 1

    def columns(j):
        return pl.ds(pl.multiple_of(j * COLS, COLS), COLS)

    def load_up(j, s):
        return [
            pltpu.make_async_copy(w.at[:, columns(j)], wb.at[s, k], wsem.at[s, k])
            for k, w in enumerate((wg_hbm, wu_hbm))
        ]

    def load_down(j, s):
        return pltpu.make_async_copy(wd_hbm.at[:, columns(j)], wb.at[s, 0, pl.ds(0, ff)], wsem.at[s, 0])

    def load_x(i):
        h = CHUNKS[i] // 2
        return [
            pltpu.make_async_copy(
                x_hbm.at[pl.ds(pl.multiple_of(starts[i] + who * h, 16), h)], xb.at[pl.ds(k * h, h)], xsem.at[k]
            )
            for k, who in enumerate((core, 1 - core))
        ]

    def send_a(i, k):
        h = pl.ds(0, CHUNKS[i] // 2)
        return pltpu.make_async_remote_copy(
            out_a.at[k, h], in_a.at[TILES * i + k, h], sa.at[k], ra.at[TILES * i + k],
            device_id=sibling, device_id_type=MESH,
        )

    def send_b(i, k):
        h = pl.ds(0, CHUNKS[i] // 2)
        return pltpu.make_async_remote_copy(
            out_b.at[k, h], in_b.at[TILES * i + k, h], sb.at[k], rb.at[TILES * i + k],
            device_id=partner, device_id_type=MESH,
        )

    def y_at(i, k):
        h = CHUNKS[i] // 2
        return y_hbm.at[pl.ds(pl.multiple_of(starts[i] + core * h, 16), h), columns(k)]

    def send_y(i, k):
        return pltpu.make_async_remote_copy(
            yb.at[k, pl.ds(0, CHUNKS[i] // 2)], y_at(i, k), sy.at[k], ry.at[TILES * i + k],
            device_id=sibling, device_id_type=MESH,
        )

    def store_y(i, k):
        return pltpu.make_async_copy(yb.at[k, pl.ds(0, CHUNKS[i] // 2)], y_at(i, k), ly.at[k])

    def chip_sum(i, k, tile, slot):
        h = CHUNKS[i] // 2
        out_b[slot, :h] = (own[lax.rem(k, 4), :h] + in_a[tile, :h].astype(F32)).astype(BF16)

    def finish(i, k):
        h = CHUNKS[i] // 2
        yb[k, :h] = (out_b[k, :h].astype(F32) + in_b[TILES * i + k, :h].astype(F32)).astype(BF16)

    def wait_y(i):
        for k in range(TILES):
            send_y(i, k).wait_send()
            store_y(i, k).wait()

    barrier = pltpu.get_barrier_semaphore()
    for other in (sibling, partner):
        pl.semaphore_signal(barrier, inc=1, device_id=other, device_id_type=MESH)
    for c in load_up(0, 0) + load_x(0):
        c.start()

    for i, rows in enumerate(CHUNKS):
        h = rows // 2
        base = i * (ups + TILES)
        for c in load_x(i):
            c.wait()

        def up_step(j, carry, i=i, rows=rows, base=base):
            s = lax.rem(base + j, 2)
            for c in load_up(j, s):
                c.wait()

            @pl.when(j + 1 < ups)
            def _():
                for c in load_up(j + 1, 1 - s):
                    c.start()

            @pl.when(j + 1 == ups)
            def _():
                load_down(0, 1 - s).start()

            if i > 0:
                @pl.when(j == 1)
                def _():
                    for k in (TILES - 2, TILES - 1):
                        send_a(i - 1, k).wait_recv()
                        if i > 1:
                            send_b(i - 2, k).wait_send()
                        chip_sum(i - 1, k, TILES * (i - 1) + k, k)
                        send_b(i - 1, k).start()

            x = xb[:rows]
            gate = jnp.dot(x, wb[s, 0], preferred_element_type=F32)
            up = jnp.dot(x, wb[s, 1], preferred_element_type=F32)
            hid[:rows, columns(j)] = (jax.nn.silu(gate) * up).astype(BF16)
            return carry

        lax.fori_loop(0, ups, up_step, 0)

        if i == 0:
            pl.semaphore_wait(barrier, 2)
        if i < last:
            for c in load_x(i + 1):
                c.start()
        if i > 0:
            for k in range(TILES):
                send_a(i - 1, k).wait_send()
        if i > 1:
            wait_y(i - 2)

        def down_step(j, carry, i=i, rows=rows, base=base, h=h):
            s = lax.rem(base + ups + j, 2)
            load_down(j, s).wait()

            @pl.when(j + 1 < TILES)
            def _():
                load_down(j + 1, 1 - s).start()

            if i < last:
                @pl.when(j + 1 == TILES)
                def _():
                    for c in load_up(0, 1 - s):
                        c.start()

            @pl.when(j >= 2)
            def _():
                send_a(i, j - 2).wait_recv()
                if i > 0:
                    send_b(i - 1, j - 2).wait_send()

            if i > 0:
                send_b(i - 1, j).wait_recv()

            term = jnp.dot(hid[:rows], wb[s, 0, :ff], preferred_element_type=F32)
            tile = lax.rem(TILES * i + j - 2 + TILES * len(CHUNKS), TILES * len(CHUNKS))
            chip_sum(i, lax.rem(j + TILES - 2, TILES), tile, lax.rem(j + TILES, TILES + 2))
            if i > 0:
                finish(i - 1, j)
            own[lax.rem(j, 4), :h] = term[:h]
            out_a[j, :h] = term[h:].astype(BF16)

            @pl.when(j >= 2)
            def _():
                send_b(i, j - 2).start()

            if i > 0:
                send_y(i - 1, j).start()
                store_y(i - 1, j).start()
            send_a(i, j).start()
            return carry

        lax.fori_loop(0, TILES, down_step, 0)

    for k in (TILES - 2, TILES - 1):
        send_a(last, k).wait_recv()
        send_b(last - 1, k).wait_send()
        chip_sum(last, k, TILES * last + k, k)
        send_b(last, k).start()
    wait_y(last - 1)
    for k in range(TILES):
        send_b(last, k).wait_recv()
        finish(last, k)
        send_y(last, k).start()
        store_y(last, k).start()
    for k in range(TILES):
        send_a(last, k).wait_send()
        send_b(last, k).wait_send()
    wait_y(last)
    for i in range(len(CHUNKS)):
        for k in range(TILES):
            send_y(i, k).wait_recv()


def solution(mesh):
    def step(x, w_gate, w_up, w_down):
        rows, depth = x.shape
        ff = w_gate.shape[1]
        most, tiles = max(CHUNKS), TILES * len(CHUNKS)
        h = most // 2
        return pl.pallas_call(
            kernel,
            out_shape=jax.ShapeDtypeStruct((rows, depth), BF16),
            in_specs=[pl.BlockSpec(memory_space=pl.ANY)] * 4,
            out_specs=pl.BlockSpec(memory_space=pl.ANY),
            scratch_shapes=[
                pltpu.VMEM((most, depth), BF16),
                pltpu.VMEM((2, 2, depth, COLS), BF16),
                pltpu.VMEM((most, ff), BF16),
                pltpu.VMEM((4, h, COLS), F32),
                pltpu.VMEM((TILES, h, COLS), BF16),
                pltpu.VMEM((tiles, h, COLS), BF16),
                pltpu.VMEM((TILES + 2, h, COLS), BF16),
                pltpu.VMEM((tiles, h, COLS), BF16),
                pltpu.VMEM((TILES, h, COLS), BF16),
                pltpu.SemaphoreType.DMA((2,)),
                pltpu.SemaphoreType.DMA((2, 2)),
                pltpu.SemaphoreType.DMA((TILES,)),
                pltpu.SemaphoreType.DMA((tiles,)),
                pltpu.SemaphoreType.DMA((TILES,)),
                pltpu.SemaphoreType.DMA((tiles,)),
                pltpu.SemaphoreType.DMA((TILES,)),
                pltpu.SemaphoreType.DMA((tiles,)),
                pltpu.SemaphoreType.DMA((TILES,)),
            ],
            compiler_params=pltpu.CompilerParams(
                collective_id=0, has_side_effects=True, vmem_limit_bytes=67043328
            ),
            name="mlp",
        )(x, w_gate, w_up, w_down)

    return jax.shard_map(
        step,
        mesh=mesh,
        in_specs=(P("dp", None), P(None, "tp"), P(None, "tp"), P("tp", None)),
        out_specs=P("dp", None),
        check_vma=False,
    )
```

time: 531 us -> 263 us (0.50)
  waiting for transfers between devices: 286 us -> 0 us
  Pallas kernels: 0 us -> 249 us
  matrix products: 218 us -> 0 us
  between operations: 13.4 us -> 0.01 us
    psum x1 -> x0, waiting for transfers between devices: 286 us -> none  [step(): return lax.psum(term, 'tp')]
    pallas_call x0 -> x1, Pallas kernels: none -> 249 us  [step(): pl.pallas_call(kernel, out_shape=jax.ShapeDtypeStruct((rows, depth), BF16...]
    dot_general x3 -> x0, matrix products: 218 us -> none  [the longest x1 76.9 us: step(): up = jnp.dot(x, w_up, preferred_element_type=jnp.float32)]
  transfers between devices with their start and end apart: 1 -> 0, of which waited for: 1 -> 0; matrix products, arithmetic and copies ran while one was open for 0% -> 0% of each run, Pallas kernels for 0% -> 0%
where the time goes in v1:
time: 263 us
  Pallas kernels  249 us (95%)
  local copies, waits for them, and re-layouts  14.1 us (5%)
    pallas_call x1, Pallas kernels, step(): pl.pallas_call(kernel, out_shape=jax.ShapeDtypeStruct((rows, depth), BF16...  249 us
    unnamed x1, local copies, waits for them, and re-layouts  14.1 us

profile of v1, /device:TPU:0, one launch (start us, length us, event | category | flops | bytes accessed | tf_op | source)
XLA Modules:
  0.0 262.8 jit_solution(15991848335653084894)
XLA Ops:
  0.0 248.8 %mlp.1 = bf16[2048,4096]{1,0:T(8,128)(2,1)} custom-call(bf16[2048,4096]{1,0:T(8,128)(2,1)} %x_hbm.1, bf16[4096,3584]{1,0:T(8,128)(2,1)} %wg_hbm.1, bf16[4096,3584]{1,0:T(8,128)(2,1)} %wu_hbm.1, bf16[3584,4096]{1,0:T(8,128)(2,1)} %wd_hbm.1), custom_call_target="tpu_custom_call" | custom-call | tf_op jit(solution)/shard_map/mlp/pallas_call | solution.py:216
  248.8 14.1 %copy.6 = bf16[2048,4096]{1,0:T(8,128)(2,1)} copy(bf16[2048,4096]{1,0:T(8,128)(2,1)} %mlp.1) | data formatting | bytes 33554432

commit v2 on v1

v2 whole, which is shorter than its diff:
```python
import functools

import jax
import jax.numpy as jnp
from jax import lax
from jax.experimental import pallas as pl
from jax.experimental.pallas import tpu as pltpu
from jax.sharding import PartitionSpec as P

MESH = pl.DeviceIdType.MESH
BF16, F32 = jnp.bfloat16, jnp.float32
CHUNKS = (384, 384, 384, 320, 320, 256)
COLS = 512
TILES = 4
SLOTS = 3
COPIES = 16


def kernel(
    x_hbm, wg_hbm, wu_hbm, wd_hbm, y_hbm,
    xb, wb, hid, own, out_a, in_a, out_b, in_b, yb,
    xsem, wsem, sa, ra, sb, rb, sy, ry, ly,
):
    depth, ff = wg_hbm.shape
    ups = ff // COLS
    dp, tp = lax.axis_index("dp"), lax.axis_index("tp")
    chip, core = tp // 2, tp % 2
    sibling = (dp, 2 * chip + 1 - core)
    partner = (dp, 2 * (1 - chip) + core)
    starts = [sum(CHUNKS[:i]) for i in range(len(CHUNKS))]
    last = len(CHUNKS) - 1

    def columns(j):
        return pl.ds(pl.multiple_of(j * COLS, COLS), COLS)

    def load_up(j, s):
        return [
            pltpu.make_async_copy(w.at[:, columns(j)], wb.at[s, k], wsem.at[s, k])
            for k, w in enumerate((wg_hbm, wu_hbm))
        ]

    def load_down(j, s):
        return [
            pltpu.make_async_copy(wd_hbm.at[:, columns(2 * j + k)], wb.at[s, k, pl.ds(0, ff)], wsem.at[s, k])
            for k in range(2)
        ]

    def load_x(i):
        h = CHUNKS[i] // 2
        return [
            pltpu.make_async_copy(
                x_hbm.at[pl.ds(pl.multiple_of(starts[i] + who * h, 16), h)], xb.at[pl.ds(k * h, h)], xsem.at[k]
            )
            for k, who in enumerate((core, 1 - core))
        ]

    def send_a(i, k):
        h = pl.ds(0, CHUNKS[i] // 2)
        return pltpu.make_async_remote_copy(
            out_a.at[k, h], in_a.at[k, h], sa.at[k], ra.at[k],
            device_id=sibling, device_id_type=MESH,
        )

    def send_b(i, k):
        h = pl.ds(0, CHUNKS[i] // 2)
        return pltpu.make_async_remote_copy(
            out_b.at[k, h], in_b.at[TILES * (i % 2) + k, h], sb.at[k], rb.at[TILES * (i % 2) + k],
            device_id=partner, device_id_type=MESH,
        )

    def y_at(i, k):
        h = CHUNKS[i] // 2
        return y_hbm.at[pl.ds(pl.multiple_of(starts[i] + core * h, 16), h), pl.ds(pl.multiple_of(2 * COLS * k, COLS), 2 * COLS)]

    def send_y(i, k):
        return pltpu.make_async_remote_copy(
            yb.at[k, pl.ds(0, CHUNKS[i] // 2)], y_at(i, k), sy.at[k], ry.at[TILES * i + k],
            device_id=sibling, device_id_type=MESH,
        )

    def store_y(i, k):
        return pltpu.make_async_copy(yb.at[k, pl.ds(0, CHUNKS[i] // 2)], y_at(i, k), ly.at[k])

    def chip_sum(i, k, slot):
        h = CHUNKS[i] // 2
        out_b[slot, :h] = (own[lax.rem(k, 2), :h] + in_a[k, :h].astype(F32)).astype(BF16)

    def finish(i, k):
        h = CHUNKS[i] // 2
        yb[k, :h] = (out_b[k, :h].astype(F32) + in_b[TILES * (i % 2) + k, :h].astype(F32)).astype(BF16)

    def wait_y(i):
        for k in range(TILES):
            send_y(i, k).wait_send()
            store_y(i, k).wait()

    barrier = pltpu.get_barrier_semaphore()
    for other in (sibling, partner):
        pl.semaphore_signal(barrier, inc=1, device_id=other, device_id_type=MESH)
    for c in load_x(0) + load_up(0, 0) + load_up(1, 1):
        c.start()

    for i, rows in enumerate(CHUNKS):
        h = rows // 2
        base = i * (ups + TILES)
        for c in load_x(i):
            c.wait()

        def up_step(j, carry, i=i, rows=rows, base=base):
            s, free = lax.rem(base + j, SLOTS), lax.rem(base + j + 2, SLOTS)
            for c in load_up(j, s):
                c.wait()

            @pl.when(j + 2 < ups)
            def _():
                for c in load_up(j + 2, free):
                    c.start()

            @pl.when(j + 2 >= ups)
            def _():
                for c in load_down(j + 2 - ups, free):
                    c.start()

            if i > 0:
                @pl.when(j == 1)
                def _():
                    k = TILES - 1
                    send_a(i - 1, k).wait_recv()
                    if i > 1:
                        send_b(i - 2, k).wait_send()
                    chip_sum(i - 1, k, k)
                    send_b(i - 1, k).start()

            x = xb[:rows]
            gate = jnp.dot(x, wb[s, 0], preferred_element_type=F32)
            up = jnp.dot(x, wb[s, 1], preferred_element_type=F32)
            hid[:rows, columns(j)] = (jax.nn.silu(gate) * up).astype(BF16)
            return carry

        lax.fori_loop(0, ups, up_step, 0)

        if i == 0:
            pl.semaphore_wait(barrier, 2)
        if i < last:
            for c in load_x(i + 1):
                c.start()
        if i > 0:
            for k in range(TILES):
                send_a(i - 1, k).wait_send()
        if i > 1:
            wait_y(i - 2)

        def down_step(j, carry, i=i, rows=rows, base=base, h=h):
            s, free = lax.rem(base + ups + j, SLOTS), lax.rem(base + ups + j + 2, SLOTS)
            for c in load_down(j, s):
                c.wait()

            @pl.when(j + 2 < TILES)
            def _():
                for c in load_down(j + 2, free):
                    c.start()

            if i < last:
                @pl.when(j + 2 >= TILES)
                def _():
                    for c in load_up(j + 2 - TILES, free):
                        c.start()

            if i > 0:
                send_b(i - 1, j).wait_recv()

            def half(k):
                term = jnp.dot(hid[:rows], wb[s, k, :ff], preferred_element_type=F32)
                own[lax.rem(j, 2), :h, pl.ds(k * COLS, COLS)] = term[:h]
                out_a[j, :h, pl.ds(k * COLS, COLS)] = term[h:].astype(BF16)

            half(0)
            if i > 0:
                finish(i - 1, j)

            half(1)

            @pl.when(j >= 1)
            def _():
                send_a(i, j - 1).wait_recv()
                if i > 0:
                    send_b(i - 1, j - 1).wait_send()

            chip_sum(i, lax.rem(j + TILES - 1, TILES), lax.rem(j + TILES, TILES + 1))

            @pl.when(j >= 1)
            def _():
                send_b(i, j - 1).start()

            if i > 0:
                send_y(i - 1, j).start()
                store_y(i - 1, j).start()
            send_a(i, j).start()
            return carry

        lax.fori_loop(0, TILES, down_step, 0)

    send_a(last, TILES - 1).wait_recv()
    send_b(last - 1, TILES - 1).wait_send()
    chip_sum(last, TILES - 1, TILES - 1)
    send_b(last, TILES - 1).start()
    wait_y(last - 1)
    for k in range(TILES):
        send_b(last, k).wait_recv()
        finish(last, k)
        send_y(last, k).start()
        store_y(last, k).start()
    for k in range(TILES):
        send_a(last, k).wait_send()
        send_b(last, k).wait_send()
    wait_y(last)
    for i in range(len(CHUNKS)):
        for k in range(TILES):
            send_y(i, k).wait_recv()


def copy(y_hbm, out_hbm, buffer, read, written):
    rows = buffer.shape[1]

    def load(k):
        return pltpu.make_async_copy(y_hbm.at[pl.ds(k * rows, rows)], buffer.at[k], read.at[k])

    def store(k):
        return pltpu.make_async_copy(buffer.at[k], out_hbm.at[pl.ds(k * rows, rows)], written.at[k])

    for k in range(COPIES):
        load(k).start()
    for k in range(COPIES):
        load(k).wait()
        store(k).start()
    for k in range(COPIES):
        store(k).wait()


def solution(mesh):
    def step(x, w_gate, w_up, w_down):
        rows, depth = x.shape
        ff = w_gate.shape[1]
        most, tiles = max(CHUNKS), TILES * len(CHUNKS)
        h = most // 2
        y = pl.pallas_call(
            kernel,
            out_shape=jax.ShapeDtypeStruct((rows, depth), BF16),
            in_specs=[pl.BlockSpec(memory_space=pl.ANY)] * 4,
            out_specs=pl.BlockSpec(memory_space=pl.ANY),
            scratch_shapes=[
                pltpu.VMEM((most, depth), BF16),
                pltpu.VMEM((SLOTS, 2, depth, COLS), BF16),
                pltpu.VMEM((most, ff), BF16),
                pltpu.VMEM((2, h, 2 * COLS), F32),
                pltpu.VMEM((TILES, h, 2 * COLS), BF16),
                pltpu.VMEM((TILES, h, 2 * COLS), BF16),
                pltpu.VMEM((TILES + 1, h, 2 * COLS), BF16),
                pltpu.VMEM((2 * TILES, h, 2 * COLS), BF16),
                pltpu.VMEM((TILES, h, 2 * COLS), BF16),
                pltpu.SemaphoreType.DMA((2,)),
                pltpu.SemaphoreType.DMA((SLOTS, 2)),
                pltpu.SemaphoreType.DMA((TILES,)),
                pltpu.SemaphoreType.DMA((TILES,)),
                pltpu.SemaphoreType.DMA((TILES,)),
                pltpu.SemaphoreType.DMA((2 * TILES,)),
                pltpu.SemaphoreType.DMA((TILES,)),
                pltpu.SemaphoreType.DMA((tiles,)),
                pltpu.SemaphoreType.DMA((TILES,)),
            ],
            compiler_params=pltpu.CompilerParams(
                collective_id=0, has_side_effects=True, vmem_limit_bytes=67043328
            ),
            name="mlp",
        )(x, w_gate, w_up, w_down)
        return pl.pallas_call(
            copy,
            out_shape=jax.ShapeDtypeStruct((rows, depth), BF16),
            in_specs=[pl.BlockSpec(memory_space=pl.ANY)],
            out_specs=pl.BlockSpec(memory_space=pl.ANY),
            scratch_shapes=[
                pltpu.VMEM((COPIES, rows // COPIES, depth), BF16),
                pltpu.SemaphoreType.DMA((COPIES,)),
                pltpu.SemaphoreType.DMA((COPIES,)),
            ],
            compiler_params=pltpu.CompilerParams(vmem_limit_bytes=67043328),
            name="result",
        )(y)

    return jax.shard_map(
        step,
        mesh=mesh,
        in_specs=(P("dp", None), P(None, "tp"), P(None, "tp"), P("tp", None)),
        out_specs=P("dp", None),
        check_vma=False,
    )
```

time: 263 us -> 242 us (0.920)
  local copies, waits for them, and re-layouts: 14.1 us -> 0 us
  Pallas kernels: 249 us -> 241 us
    pallas_call x1, Pallas kernels: 249 us -> 229 us  [step(): pl.pallas_call(kernel, out_shape=jax.ShapeDtypeStruct((rows, depth), BF16...]
    unnamed x1 -> x0, local copies, waits for them, and re-layouts: 14.1 us -> none
    pallas_call x0 -> x1, Pallas kernels: none -> 12 us  [step(): pl.pallas_call(copy, out_shape=jax.ShapeDtypeStruct((rows, depth), BF16),...]
where the time goes in v2:
time: 242 us
  Pallas kernels  241 us (100%)
    pallas_call x1, Pallas kernels, step(): pl.pallas_call(kernel, out_shape=jax.ShapeDtypeStruct((rows, depth), BF16...  229 us
    pallas_call x1, Pallas kernels, step(): pl.pallas_call(copy, out_shape=jax.ShapeDtypeStruct((rows, depth), BF16),...  12 us

profile of v2, /device:TPU:0, one launch (start us, length us, event | category | flops | bytes accessed | tf_op | source)
XLA Modules:
  0.0 241.6 jit_solution(9784653699611511644)
XLA Ops:
  0.0 229.4 %mlp.1.y_hbm = bf16[2048,4096]{1,0:T(8,128)(2,1)} custom-call(bf16[2048,4096]{1,0:T(8,128)(2,1)} %x_hbm.1, bf16[4096,3584]{1,0:T(8,128)(2,1)} %wg_hbm.1, bf16[4096,3584]{1,0:T(8,128)(2,1)} %wu_hbm.1, bf16[3584,4096]{1,0:T(8,128)(2,1)} %wd_hbm.1), custom_call_target="tpu_custom_call" | custom-call | tf_op jit(solution)/shard_map/mlp/pallas_call | solution.py:246
  229.4 12.0 %result.1 = bf16[2048,4096]{1,0:T(8,128)(2,1)} custom-call(bf16[2048,4096]{1,0:T(8,128)(2,1)} %mlp.1.y_hbm), custom_call_target="tpu_custom_call" | custom-call | tf_op jit(solution)/shard_map/result/pallas_call | solution.py:276

commit v3 on v2

--- a/solution.py
+++ b/solution.py
@@ -17,9 +17,9 @@
 
 
 def kernel(
-    x_hbm, wg_hbm, wu_hbm, wd_hbm, y_hbm,
-    xb, wb, hid, own, out_a, in_a, out_b, in_b, yb,
-    xsem, wsem, sa, ra, sb, rb, sy, ry, ly,
+    x_hbm, wg_hbm, wu_hbm, wd_hbm, y_ref,
+    xb, wb, hid, own, out_a, in_a, out_b, in_b,
+    xsem, wsem, sa, ra, sb, rb, sy, ry,
 ):
     depth, ff = wg_hbm.shape
     ups = ff // COLS
@@ -70,29 +70,24 @@
 
     def y_at(i, k):
         h = CHUNKS[i] // 2
-        return y_hbm.at[pl.ds(pl.multiple_of(starts[i] + core * h, 16), h), pl.ds(pl.multiple_of(2 * COLS * k, COLS), 2 * COLS)]
+        return (
+            pl.ds(pl.multiple_of(starts[i] + core * h, 32), h),
+            pl.ds(pl.multiple_of(2 * COLS * k, COLS), 2 * COLS),
+        )
 
     def send_y(i, k):
         return pltpu.make_async_remote_copy(
-            yb.at[k, pl.ds(0, CHUNKS[i] // 2)], y_at(i, k), sy.at[k], ry.at[TILES * i + k],
+            y_ref.at[*y_at(i, k)], y_ref.at[*y_at(i, k)], sy.at[TILES * i + k], ry.at[TILES * i + k],
             device_id=sibling, device_id_type=MESH,
         )
 
-    def store_y(i, k):
-        return pltpu.make_async_copy(yb.at[k, pl.ds(0, CHUNKS[i] // 2)], y_at(i, k), ly.at[k])
-
     def chip_sum(i, k, slot):
         h = CHUNKS[i] // 2
         out_b[slot, :h] = (own[lax.rem(k, 2), :h] + in_a[k, :h].astype(F32)).astype(BF16)
 
     def finish(i, k):
         h = CHUNKS[i] // 2
-        yb[k, :h] = (out_b[k, :h].astype(F32) + in_b[TILES * (i % 2) + k, :h].astype(F32)).astype(BF16)
-
-    def wait_y(i):
-        for k in range(TILES):
-            send_y(i, k).wait_send()
-            store_y(i, k).wait()
+        y_ref[*y_at(i, k)] = (out_b[k, :h].astype(F32) + in_b[TILES * (i % 2) + k, :h].astype(F32)).astype(BF16)
 
     barrier = pltpu.get_barrier_semaphore()
     for other in (sibling, partner):
@@ -147,8 +142,6 @@
         if i > 0:
             for k in range(TILES):
                 send_a(i - 1, k).wait_send()
-        if i > 1:
-            wait_y(i - 2)
 
         def down_step(j, carry, i=i, rows=rows, base=base, h=h):
             s, free = lax.rem(base + ups + j, SLOTS), lax.rem(base + ups + j + 2, SLOTS)
@@ -194,7 +187,6 @@
 
             if i > 0:
                 send_y(i - 1, j).start()
-                store_y(i - 1, j).start()
             send_a(i, j).start()
             return carry
 
@@ -204,34 +196,26 @@
     send_b(last - 1, TILES - 1).wait_send()
     chip_sum(last, TILES - 1, TILES - 1)
     send_b(last, TILES - 1).start()
-    wait_y(last - 1)
     for k in range(TILES):
         send_b(last, k).wait_recv()
         finish(last, k)
         send_y(last, k).start()
-        store_y(last, k).start()
     for k in range(TILES):
         send_a(last, k).wait_send()
         send_b(last, k).wait_send()
-    wait_y(last)
     for i in range(len(CHUNKS)):
         for k in range(TILES):
-            send_y(i, k).wait_recv()
-
-
-def copy(y_hbm, out_hbm, buffer, read, written):
-    rows = buffer.shape[1]
-
-    def load(k):
-        return pltpu.make_async_copy(y_hbm.at[pl.ds(k * rows, rows)], buffer.at[k], read.at[k])
+            send_y(i, k).wait()
+
+
+def copy(y_ref, out_hbm, written):
+    rows = y_ref.shape[0] // COPIES
 
     def store(k):
-        return pltpu.make_async_copy(buffer.at[k], out_hbm.at[pl.ds(k * rows, rows)], written.at[k])
+        part = pl.ds(k * rows, rows)
+        return pltpu.make_async_copy(y_ref.at[part], out_hbm.at[part], written.at[k])
 
     for k in range(COPIES):
-        load(k).start()
-    for k in range(COPIES):
-        load(k).wait()
         store(k).start()
     for k in range(COPIES):
         store(k).wait()
@@ -245,9 +229,9 @@
         h = most // 2
         y = pl.pallas_call(
             kernel,
-            out_shape=jax.ShapeDtypeStruct((rows, depth), BF16),
+            out_shape=pltpu.VMEM((rows, depth), BF16),
             in_specs=[pl.BlockSpec(memory_space=pl.ANY)] * 4,
-            out_specs=pl.BlockSpec(memory_space=pl.ANY),
+            out_specs=pl.BlockSpec(memory_space=pltpu.VMEM),
             scratch_shapes=[
                 pltpu.VMEM((most, depth), BF16),
                 pltpu.VMEM((SLOTS, 2, depth, COLS), BF16),
@@ -257,33 +241,27 @@
                 pltpu.VMEM((TILES, h, 2 * COLS), BF16),
                 pltpu.VMEM((TILES + 1, h, 2 * COLS), BF16),
                 pltpu.VMEM((2 * TILES, h, 2 * COLS), BF16),
-                pltpu.VMEM((TILES, h, 2 * COLS), BF16),
                 pltpu.SemaphoreType.DMA((2,)),
                 pltpu.SemaphoreType.DMA((SLOTS, 2)),
                 pltpu.SemaphoreType.DMA((TILES,)),
                 pltpu.SemaphoreType.DMA((TILES,)),
                 pltpu.SemaphoreType.DMA((TILES,)),
                 pltpu.SemaphoreType.DMA((2 * TILES,)),
-                pltpu.SemaphoreType.DMA((TILES,)),
                 pltpu.SemaphoreType.DMA((tiles,)),
-                pltpu.SemaphoreType.DMA((TILES,)),
+                pltpu.SemaphoreType.DMA((tiles,)),
             ],
             compiler_params=pltpu.CompilerParams(
-                collective_id=0, has_side_effects=True, vmem_limit_bytes=67043328
+                collective_id=0, has_side_effects=True, vmem_limit_bytes=47 * 2**20
             ),
             name="mlp",
         )(x, w_gate, w_up, w_down)
         return pl.pallas_call(
             copy,
             out_shape=jax.ShapeDtypeStruct((rows, depth), BF16),
-            in_specs=[pl.BlockSpec(memory_space=pl.ANY)],
+            in_specs=[pl.BlockSpec(memory_space=pltpu.VMEM)],
             out_specs=pl.BlockSpec(memory_space=pl.ANY),
-            scratch_shapes=[
-                pltpu.VMEM((COPIES, rows // COPIES, depth), BF16),
-                pltpu.SemaphoreType.DMA((COPIES,)),
-                pltpu.SemaphoreType.DMA((COPIES,)),
-            ],
-            compiler_params=pltpu.CompilerParams(vmem_limit_bytes=67043328),
+            scratch_shapes=[pltpu.SemaphoreType.DMA((COPIES,))],
+            compiler_params=pltpu.CompilerParams(vmem_limit_bytes=24 * 2**20),
             name="result",
         )(y)
 

time: 242 us -> 236 us (0.975)
  Pallas kernels: 241 us -> 236 us
    pallas_call x1, Pallas kernels: 12 us -> 5.96 us  [step(): pl.pallas_call(copy, out_shape=jax.ShapeDtypeStruct((rows, depth), BF16),...]
where the time goes in v3:
time: 236 us
  Pallas kernels  236 us (100%)
    pallas_call x1, Pallas kernels, step(): pl.pallas_call(kernel, out_shape=pltpu.VMEM((rows, depth), BF16), in_spec...  230 us
    pallas_call x1, Pallas kernels, step(): pl.pallas_call(copy, out_shape=jax.ShapeDtypeStruct((rows, depth), BF16),...  5.96 us

profile of v3, /device:TPU:0, one launch (start us, length us, event | category | flops | bytes accessed | tf_op | source)
XLA Modules:
  0.0 235.8 jit_solution(10175658054910628826)
XLA Ops:
  0.0 229.6 %mlp.1.y_ref = bf16[2048,4096]{1,0:T(8,128)(2,1)S(1)} custom-call(bf16[2048,4096]{1,0:T(8,128)(2,1)} %x_hbm.1, bf16[4096,3584]{1,0:T(8,128)(2,1)} %wg_hbm.1, bf16[4096,3584]{1,0:T(8,128)(2,1)} %wu_hbm.1, bf16[3584,4096]{1,0:T(8,128)(2,1)} %wd_hbm.1), custom_call_target="tpu_custom_call" | custom-call | tf_op jit(solution)/shard_map/mlp/pallas_call | solution.py:230
  229.6 6.0 %result.1 = bf16[2048,4096]{1,0:T(8,128)(2,1)} custom-call(bf16[2048,4096]{1,0:T(8,128)(2,1)S(1)} %mlp.1.y_ref), custom_call_target="tpu_custom_call" | custom-call | tf_op jit(solution)/shard_map/result/pallas_call | solution.py:258

commit v4 on v3

--- a/solution.py
+++ b/solution.py
@@ -13,7 +13,7 @@
 COLS = 512
 TILES = 4
 SLOTS = 3
-COPIES = 16
+COPIES = 4
 
 
 def kernel(
@@ -92,7 +92,7 @@
     barrier = pltpu.get_barrier_semaphore()
     for other in (sibling, partner):
         pl.semaphore_signal(barrier, inc=1, device_id=other, device_id_type=MESH)
-    for c in load_x(0) + load_up(0, 0) + load_up(1, 1):
+    for c in load_x(0) + load_up(0, 0):
         c.start()
 
     for i, rows in enumerate(CHUNKS):
@@ -105,6 +105,12 @@
             s, free = lax.rem(base + j, SLOTS), lax.rem(base + j + 2, SLOTS)
             for c in load_up(j, s):
                 c.wait()
+
+            if i == 0:
+                @pl.when(j == 0)
+                def _():
+                    for c in load_up(1, 1):
+                        c.start()
 
             @pl.when(j + 2 < ups)
             def _():

time: 236 us -> 235 us (level)
  no operation moved by 1% of the time
where the time goes in v4:
time: 235 us
  Pallas kernels  234 us (100%)
    pallas_call x1, Pallas kernels, step(): pl.pallas_call(kernel, out_shape=pltpu.VMEM((rows, depth), BF16), in_spec...  228 us
    pallas_call x1, Pallas kernels, step(): pl.pallas_call(copy, out_shape=jax.ShapeDtypeStruct((rows, depth), BF16),...  5.95 us

profile of v4, /device:TPU:0, one launch (start us, length us, event | category | flops | bytes accessed | tf_op | source)
XLA Modules:
  0.0 234.6 jit_solution(4085862563913594697)
XLA Ops:
  0.0 228.4 %mlp.1.y_ref = bf16[2048,4096]{1,0:T(8,128)(2,1)S(1)} custom-call(bf16[2048,4096]{1,0:T(8,128)(2,1)} %x_hbm.1, bf16[4096,3584]{1,0:T(8,128)(2,1)} %wg_hbm.1, bf16[4096,3584]{1,0:T(8,128)(2,1)} %wu_hbm.1, bf16[3584,4096]{1,0:T(8,128)(2,1)} %wd_hbm.1), custom_call_target="tpu_custom_call" | custom-call | tf_op jit(solution)/shard_map/mlp/pallas_call | solution.py:236
  228.4 6.0 %result.1 = bf16[2048,4096]{1,0:T(8,128)(2,1)} custom-call(bf16[2048,4096]{1,0:T(8,128)(2,1)S(1)} %mlp.1.y_ref), custom_call_target="tpu_custom_call" | custom-call | tf_op jit(solution)/shard_map/result/pallas_call | solution.py:264

commit v5 on v4

--- a/solution.py
+++ b/solution.py
@@ -9,7 +9,7 @@
 
 MESH = pl.DeviceIdType.MESH
 BF16, F32 = jnp.bfloat16, jnp.float32
-CHUNKS = (384, 384, 384, 320, 320, 256)
+CHUNKS = (384, 384, 384, 352, 288, 256)
 COLS = 512
 TILES = 4
 SLOTS = 3
@@ -71,7 +71,7 @@
     def y_at(i, k):
         h = CHUNKS[i] // 2
         return (
-            pl.ds(pl.multiple_of(starts[i] + core * h, 32), h),
+            pl.ds(pl.multiple_of(starts[i] + core * h, 16), h),
             pl.ds(pl.multiple_of(2 * COLS * k, COLS), 2 * COLS),
         )
 
@@ -179,29 +179,33 @@
 
             half(1)
 
-            @pl.when(j >= 1)
-            def _():
-                send_a(i, j - 1).wait_recv()
+            if i < last:
+                @pl.when(j >= 1)
+                def _():
+                    send_a(i, j - 1).wait_recv()
+                    if i > 0:
+                        send_b(i - 1, j - 1).wait_send()
+
+                chip_sum(i, lax.rem(j + TILES - 1, TILES), lax.rem(j + TILES, TILES + 1))
+
+                @pl.when(j >= 1)
+                def _():
+                    send_b(i, j - 1).start()
+
                 if i > 0:
-                    send_b(i - 1, j - 1).wait_send()
-
-            chip_sum(i, lax.rem(j + TILES - 1, TILES), lax.rem(j + TILES, TILES + 1))
-
-            @pl.when(j >= 1)
-            def _():
-                send_b(i, j - 1).start()
-
-            if i > 0:
+                    send_y(i - 1, j).start()
+                send_a(i, j).start()
+            else:
+                send_a(i, j).start()
                 send_y(i - 1, j).start()
-            send_a(i, j).start()
+                send_b(i - 1, j).wait_send()
+                send_a(i, j).wait_recv()
+                chip_sum(i, j, j)
+                send_b(i, j).start()
             return carry
 
         lax.fori_loop(0, TILES, down_step, 0)
 
-    send_a(last, TILES - 1).wait_recv()
-    send_b(last - 1, TILES - 1).wait_send()
-    chip_sum(last, TILES - 1, TILES - 1)
-    send_b(last, TILES - 1).start()
     for k in range(TILES):
         send_b(last, k).wait_recv()
         finish(last, k)

time: 235 us -> 234 us (level)
  no operation moved by 1% of the time
where the time goes in v5:
time: 234 us
  Pallas kernels  234 us (100%)
    pallas_call x1, Pallas kernels, step(): pl.pallas_call(kernel, out_shape=pltpu.VMEM((rows, depth), BF16), in_spec...  228 us
    pallas_call x1, Pallas kernels, step(): pl.pallas_call(copy, out_shape=jax.ShapeDtypeStruct((rows, depth), BF16),...  5.95 us

profile of v5, /device:TPU:0, one launch (start us, length us, event | category | flops | bytes accessed | tf_op | source)
XLA Modules:
  0.0 233.8 jit_solution(8636354064110390176)
XLA Ops:
  0.0 227.7 %mlp.1.y_ref = bf16[2048,4096]{1,0:T(8,128)(2,1)S(1)} custom-call(bf16[2048,4096]{1,0:T(8,128)(2,1)} %x_hbm.1, bf16[4096,3584]{1,0:T(8,128)(2,1)} %wg_hbm.1, bf16[4096,3584]{1,0:T(8,128)(2,1)} %wu_hbm.1, bf16[3584,4096]{1,0:T(8,128)(2,1)} %wd_hbm.1), custom_call_target="tpu_custom_call" | custom-call | tf_op jit(solution)/shard_map/mlp/pallas_call | solution.py:240
  227.7 6.0 %result.1 = bf16[2048,4096]{1,0:T(8,128)(2,1)} custom-call(bf16[2048,4096]{1,0:T(8,128)(2,1)S(1)} %mlp.1.y_ref), custom_call_target="tpu_custom_call" | custom-call | tf_op jit(solution)/shard_map/result/pallas_call | solution.py:268
